TPU v7x, 32 devices: a whole 2x2x4 slice. The times are simulated.
32 devices in a mesh: groups: 2 (over y), store: 8 (over z, x), tensor: 2 (over core).
Axes of the slice: x: 2, y: 2, z: 4, core: 2. Of those that a mesh axis runs over, the one named last changes fastest.
Arguments:
- queries: bfloat16 [32, 8192], P(('groups', 'store'), 'tensor'), parts along dimension 0, may hold values from -200 to 200
- new_kv: bfloat16 [32, 2, 1024], P(('groups', 'store'), None, 'tensor'), parts along dimension 0, may hold values from -15 to 15
- kv_pages: bfloat16 [128, 2, 256, 1024], P(('groups', 'store'), None, None, 'tensor'), parts along dimension 0, may hold values from -15 to 15
- page_index: int32 [32, 4], P(('groups', 'store')), parts along dimension 0, may hold values from 0 to 7
- page_owner: int32 [32, 4], P(('groups', 'store')), parts along dimension 0, may hold values from 0 to 7, as said below
- seq_pages: int32 [32], P(('groups', 'store')), parts along dimension 0, may hold values from 1 to 4, as said below
Outputs:
- attended: bfloat16 [32, 8192], P(('groups', 'store'), 'tensor'), parts along dimension 0
There are 2 independent parts, one for each index of `groups`. A program takes and returns all parts, laid end to end along the dimension named above; each array names one. Nothing has to cross between parts.
Inputs may be any that keep to these rules, and one draw needn't show every extreme that they name: `page_owner`: page j of sequence s lies on store index (s // 2 + o) modulo the number of store indices, with o from 0 to 3; over the slots of the sequences of one store index, at most 2 share one o, so at most 2 live pages of those sequences lie on one store index. `seq_pages`: the sequences of store index 0 all have 4 pages.
All inputs are finite; a program needn't handle non-finite values.
Results may differ from a plain program's by a relative error of at most 0.0011.
Values may be sent and summed in bfloat16 or wider, within the bound.
A program may use at most 64 MiB of HBM per device.

v0:
```python
import jax
import jax.numpy as jnp
from jax import lax
from jax.sharding import PartitionSpec as P

HEAD_DIM = 128
REACH = 4


def shifted(value, axis, steps):
    count = lax.axis_size(axis)
    pairs = [(source, (source + steps) % count) for source in range(count)]
    return lax.ppermute(value, axis, pairs)


def page_partial(query_rows, served, scale):
    slots, _, length, width = served.shape
    kv_count = query_rows.shape[1]
    keys = served[:, 0].reshape(slots, length, kv_count, width // kv_count)
    values = served[:, 1].reshape(slots, length, kv_count, width // kv_count)
    scores = (
        jnp.einsum("ckgd,cpkd->ckgp", query_rows, keys, preferred_element_type=jnp.float32) * scale
    )
    peak = jnp.max(scores, axis=-1)
    weights = jnp.exp(scores - peak[..., None])
    total = jnp.sum(weights, axis=-1)
    summed = jnp.einsum(
        "ckgp,cpkd->ckgd", weights, values.astype(jnp.float32), precision=lax.Precision.HIGHEST
    )
    return (peak, total, summed)


def slot_plan(places_table, owner_table, length_table, anchor, step, count, capacity):
    seq_count, most_pages = places_table.shape
    entries = seq_count * most_pages
    positions = jnp.arange(entries, dtype=jnp.int32)
    sequence_lookup = positions // most_pages
    live = positions % most_pages < jnp.repeat(length_table, most_pages)
    page_starts = jnp.mod(owner_table.reshape(-1) - anchor, count)
    chosen = live & (page_starts == step)
    rank = jnp.cumsum(chosen.astype(jnp.int32)) - 1
    slot_numbers = jnp.arange(capacity, dtype=jnp.int32)
    picker = (chosen[None, :] & (rank[None, :] == slot_numbers[:, None])).astype(jnp.int32)
    used = jnp.sum(picker, axis=1)
    wanted = jnp.sum(picker * places_table.reshape(-1)[None, :], axis=1)
    seq_slot = jnp.sum(picker * sequence_lookup[None, :], axis=1)
    return (wanted, used, seq_slot)


def body(queries, new_kv, kv_pages, page_index, page_owner, seq_pages):
    count = lax.axis_size("store")
    myself = lax.axis_index("store")
    seq_count, most_pages = page_index.shape
    kv_count = new_kv.shape[2] // HEAD_DIM
    heads_per_group = queries.shape[1] // (kv_count * HEAD_DIM)
    entries = seq_count * most_pages
    capacity = entries // REACH
    scale = HEAD_DIM ** (-0.5)
    query_head_count = queries.reshape(seq_count, kv_count, heads_per_group, HEAD_DIM)
    peaks, totals, sums, slot_seqs, slot_used = ([], [], [], [], [])
    for step in range(REACH):
        wanted, used, seq_slot = slot_plan(
            page_index, page_owner, seq_pages, myself, step, count, capacity
        )
        query_rows = query_head_count[seq_slot]
        if step == 0:
            incoming = jnp.stack([wanted, used])
        else:
            incoming = shifted(jnp.stack([wanted, used]), "store", step)
        served = kv_pages[incoming[0]]
        if step == 0:
            partial_value = page_partial(query_rows, served, scale)
        else:
            foreign_shard_rows = shifted(query_rows, "store", step)
            partial_value = page_partial(foreign_shard_rows, served, scale)
            partial_value = shifted(
                (partial_value[0], partial_value[1], partial_value[2]), "store", -step
            )
        peaks.append(partial_value[0])
        totals.append(partial_value[1])
        sums.append(partial_value[2])
        slot_seqs.append(seq_slot)
        slot_used.append(used)
    peak = jnp.concatenate(peaks, axis=0)
    total = jnp.concatenate(totals, axis=0)
    summed = jnp.concatenate(sums, axis=0)
    member = (
        jnp.concatenate(slot_seqs)[None, :] == jnp.arange(seq_count, dtype=jnp.int32)[:, None]
    ) & (jnp.concatenate(slot_used)[None, :] > 0)
    fresh_key_rows = new_kv[:, 0].reshape(seq_count, kv_count, HEAD_DIM)
    new_values = new_kv[:, 1].reshape(seq_count, kv_count, HEAD_DIM).astype(jnp.float32)
    own = (
        jnp.einsum(
            "esnu,esu->esn", query_head_count, fresh_key_rows, preferred_element_type=jnp.float32
        )
        * scale
    )
    inside = member[:, :, None, None]
    highest = jnp.max(jnp.where(inside, peak[None], jnp.float32(-1e30)), axis=1)
    highest = jnp.maximum(highest, own)
    factor = jnp.where(
        inside, jnp.exp(jnp.where(inside, peak[None] - highest[:, None], 0.0)), jnp.float32(0.0)
    )
    own_weight = jnp.exp(own - highest)
    denominator = (
        jnp.einsum("bskg,skg->bkg", factor, total, precision=lax.Precision.HIGHEST) + own_weight
    )
    numerator = jnp.einsum("bskg,skgd->bkgd", factor, summed, precision=lax.Precision.HIGHEST)
    numerator = numerator + own_weight[..., None] * new_values[:, :, None, :]
    return (numerator / denominator[..., None]).reshape(seq_count, -1).astype(jnp.bfloat16)


def solution(mesh):
    in_specs = (
        P(("groups", "store"), "tensor"),
        P(("groups", "store"), None, "tensor"),
        P(("groups", "store"), None, None, "tensor"),
        P(("groups", "store"), None),
        P(("groups", "store"), None),
        P(("groups", "store")),
    )
    out_specs = P(("groups", "store"), "tensor")
    return jax.shard_map(body, mesh=mesh, in_specs=in_specs, out_specs=out_specs, check_vma=False)
```

profile of v0, /device:TPU:0, one launch (start us, length us, event | category | flops | bytes accessed | tf_op | source)
XLA Modules:
  0.0 62.0 jit_solution(17500604046748010121)
XLA Ops:
  0.0 0.7 %broadcast_subtract_fusion = s32[2,4]{1,0:T(2,128)S(1)} fusion(s32[2,4]{1,0:T(2,128)} %param.10, s32[]{:T(128)S(6)} %axis_index.15), kind=kLoop, calls=%fused_computation.126 | loop fusion | flops 8 | bytes 68 | tf_op jit(solution)/shard_map/sub | solution.py:39
  0.7 0.1 sub.142
  0.9 0.7 %broadcast_in_dim.23 = s32[2,4]{1,0:T(2,128)S(1)} broadcast(s32[2]{0:T(128)} %param.11), dimensions={0} | broadcast | bytes 40 | tf_op jit(solution)/shard_map/broadcast_in_dim | solution.py:38
  1.6 0.1 reshape.570
  1.7 0.8 %mul.93 = s32[8]{0:T(128)S(1)} reshape(s32[2,4]{1,0:T(2,128)} %param.9) | data formatting | bytes 64 | tf_op jit(solution)/shard_map/mul | solution.py:45
  2.5 0.2 reduce-window.35
  2.7 0.2 reduce-window.34
  2.9 0.2 reduce-window.33
  3.1 0.2 reduce-window.32
  3.3 0.3 convert_reduce_fusion
  3.6 4.0 %collective-permute-start.7 = (s32[2,2]{1,0:T(2,128)S(1)}, s32[2,2]{1,0:T(2,128)S(1)}, u32[]{:S(2)}, u32[]{:S(2)}) collective-permute-start(s32[2,2]{1,0:T(2,128)S(1)} %pad_add_fusion.2), channel_id=1, source_target_pairs={{0,6},{2,8},{4,10},{6,12},{8,14},{10,0},{12,2},{14,4},{1,7},{3,9},... | collective-permute-start | bytes 56 | tf_op jit(solution)/shard_map/ppermute | solution.py:13
  7.7 1.6 %collective-permute-start.4 = (s32[2,2]{1,0:T(2,128)S(1)}, s32[2,2]{1,0:T(2,128)S(1)}, u32[]{:S(2)}, u32[]{:S(2)}) collective-permute-start(s32[2,2]{1,0:T(2,128)S(1)} %pad_add_fusion.1), channel_id=1, source_target_pairs={{0,4},{2,6},{4,8},{6,10},{8,12},{10,14},{12,0},{14,2},{1,5},{3,7},... | collective-permute-start | bytes 56 | tf_op jit(solution)/shard_map/ppermute | solution.py:13
  9.2 1.5 %collective-permute-start.1 = (s32[2,2]{1,0:T(2,128)S(1)}, s32[2,2]{1,0:T(2,128)S(1)}, u32[]{:S(2)}, u32[]{:S(2)}) collective-permute-start(s32[2,2]{1,0:T(2,128)S(1)} %pad_add_fusion), channel_id=1, source_target_pairs={{0,2},{2,4},{4,6},{6,8},{8,10},{10,12},{12,14},{14,0},{1,3},{3,5},... | collective-permute-start | bytes 56 | tf_op jit(solution)/shard_map/ppermute | solution.py:13
  10.8 0.7 %copy.80 = bf16[1,2,32,128]{3,2,1,0:T(8,128)(2,1)S(1)} copy(bf16[1,2,32,128]{3,1,2,0:T(2,128)(2,1)} %bitcast.115) | data formatting | bytes 32768
  11.5 0.6 gather_fusion.2
  12.1 1.5 %collective-permute-start = (bf16[2,4,8,128]{3,2,1,0:T(8,128)(2,1)S(1)}, bf16[2,4,8,128]{3,2,1,0:T(8,128)(2,1)S(1)}, u32[]{:S(2)}, u32[]{:S(2)}) collective-permute-start(bf16[2,4,8,128]{3,2,1,0:T(8,128)(2,1)S(1)} %gather_fusion.2), channel_id=1, source_target_pairs={{0,2},{2,4},{4,6},{6,8},{8,10},{10,12},{12,14},{14,0},{1,3},{3,5},... | collective-permute-start | bytes 49160 | tf_op jit(solution)/shard_map/ppermute | solution.py:13
  13.6 0.6 gather_fusion.4
  14.2 0.3 collective-permute-start.3
  14.5 0.7 %slice_convert_fusion = f32[2,1,512]{2,1,0:T(1,128)S(1)} fusion(bf16[2,2,512]{2,1,0:T(2,128)(2,1)} %param.7), kind=kLoop, calls=%fused_computation.59 | loop fusion | flops 1024 | bytes 6144 | tf_op jit(solution)/shard_map/convert_element_type | solution.py:91
  15.2 0.8 %fusion.24 = f32[2,4,1,8]{3,2,1,0:T(1,128)S(1)} fusion(bf16[2,4,8,128]{3,2,1,0:T(8,128)(2,1)S(1)} %bitcast.111, bf16[2,2,512]{2,1,0:T(2,128)(2,1)} %param.7), kind=kOutput, calls=%fused_computation.57 | convolution fusion | flops 16384 | bytes 20736 | tf_op jit(solution)/shard_map/esnu,esu->esn/dot_general | solution.py:93
  16.2 0.1 copy.73
  16.3 0.6 gather_fusion.6
  16.8 0.6 gather_fusion
  17.4 2.8 %gather_fusion.1 = bf16[2,2,256,512]{3,2,1,0:T(8,128)(2,1)S(1)} fusion(bf16[8,2,256,512]{3,2,1,0:T(8,128)(2,1)} %param.8, s32[1024]{0:T(1024)S(1)} %pad_clamp_fusion.6), kind=kCustom, calls=%fused_computation.1 | custom fusion | bytes 2097160 | tf_op jit(solution)/shard_map/gather | solution.py:70
  20.3 0.2 copy.45
  20.5 0.2 copy.47
  20.7 0.3 fusion.51
  21.0 0.2 fusion.4
  21.1 0.6 fusion.5
  21.7 2.6 %collective-permute-start.6 = (bf16[2,4,8,128]{3,2,1,0:T(8,128)(2,1)S(1)}, bf16[2,4,8,128]{3,2,1,0:T(8,128)(2,1)S(1)}, u32[]{:S(2)}, u32[]{:S(2)}) collective-permute-start(bf16[2,4,8,128]{3,2,1,0:T(8,128)(2,1)S(1)} %gather_fusion.6), channel_id=1, source_target_pairs={{0,6},{2,8},{4,10},{6,12},{8,14},{10,0},{12,2},{14,4},{1,7},{3,9},... | collective-permute-start | bytes 49160 | tf_op jit(solution)/shard_map/ppermute | solution.py:13
  24.4 2.8 %gather_fusion.3 = bf16[2,2,256,512]{3,2,1,0:T(8,128)(2,1)S(1)} fusion(bf16[8,2,256,512]{3,2,1,0:T(8,128)(2,1)} %param.8, s32[1024]{0:T(1024)S(1)} %pad_clamp_fusion.4), kind=kCustom, calls=%fused_computation.3 | custom fusion | bytes 2097160 | tf_op jit(solution)/shard_map/gather | solution.py:70
  27.3 2.8 %gather_fusion.5 = bf16[2,2,256,512]{3,2,1,0:T(8,128)(2,1)S(1)} fusion(bf16[8,2,256,512]{3,2,1,0:T(8,128)(2,1)} %param.8, s32[1024]{0:T(1024)S(1)} %pad_clamp_fusion.2), kind=kCustom, calls=%fused_computation.5 | custom fusion | bytes 2097160 | tf_op jit(solution)/shard_map/gather | solution.py:70
  30.1 1.1 %fusion.46 = (bf16[2,1,256,512]{3,2,1,0:T(8,128)(2,1)}, bf16[2,1,256,512]{3,2,1,0:T(8,128)(2,1)}) fusion(bf16[2,2,256,512]{3,2,1,0:T(8,128)(2,1)S(1)} %gather_fusion.5), kind=kLoop, calls=%fused_computation.133 | loop fusion | bytes 2097152 | tf_op jit(solution)/shard_map/slice | solution.py:19
  31.2 2.8 %gather_fusion.7 = bf16[2,2,256,512]{3,2,1,0:T(8,128)(2,1)S(1)} fusion(bf16[8,2,256,512]{3,2,1,0:T(8,128)(2,1)} %param.8, s32[1024]{0:T(1024)S(1)} %pad_clamp_fusion), kind=kCustom, calls=%fused_computation.7 | custom fusion | bytes 2097160 | tf_op jit(solution)/shard_map/gather | solution.py:70
  34.0 1.1 %fusion.47 = (bf16[2,1,256,512]{3,2,1,0:T(8,128)(2,1)}, bf16[2,1,256,512]{3,2,1,0:T(8,128)(2,1)}) fusion(bf16[2,2,256,512]{3,2,1,0:T(8,128)(2,1)S(1)} %gather_fusion.7), kind=kLoop, calls=%fused_computation.134 | loop fusion | bytes 2097152 | tf_op jit(solution)/shard_map/slice | solution.py:19
  35.1 0.2 copy.49
  35.3 0.2 copy.51
  35.5 1.2 %copy.53 = bf16[2,1,256,512]{2,3,0,1:T(8,128)(2,1)S(1)} copy(bf16[2,1,256,512]{3,2,1,0:T(8,128)(2,1)} %get-tuple-element.29) | data formatting | bytes 1048576 | tf_op jit(solution)/shard_map/slice | solution.py:19
  36.8 1.2 %copy.55 = bf16[2,1,256,512]{2,3,0,1:T(8,128)(2,1)S(1)} copy(bf16[2,1,256,512]{3,2,1,0:T(8,128)(2,1)} %get-tuple-element.30) | data formatting | bytes 1048576 | tf_op jit(solution)/shard_map/slice | solution.py:20
  38.0 1.2 %copy.57 = bf16[2,1,256,512]{2,3,0,1:T(8,128)(2,1)S(1)} copy(bf16[2,1,256,512]{3,2,1,0:T(8,128)(2,1)} %get-tuple-element.31) | data formatting | bytes 1048576 | tf_op jit(solution)/shard_map/slice | solution.py:19
  39.3 1.2 %copy.59 = bf16[2,1,256,512]{2,3,0,1:T(8,128)(2,1)S(1)} copy(bf16[2,1,256,512]{3,2,1,0:T(8,128)(2,1)} %get-tuple-element.32) | data formatting | bytes 1048576 | tf_op jit(solution)/shard_map/slice | solution.py:20
  40.5 0.3 fusion.50
  40.8 2.3 %collective-permute-start.9 = (f32[2,4,8]{2,1,0:T(4,128)S(1)}, f32[2,4,8]{2,1,0:T(4,128)S(1)}, u32[]{:S(2)}, u32[]{:S(2)}) collective-permute-start(f32[2,4,8]{2,1,0:T(4,128)S(1)} %get-tuple-element.43), channel_id=1, source_target_pairs={{0,14},{2,0},{4,2},{6,4},{8,6},{10,8},{12,10},{14,12},{1,15},{3,1}... | collective-permute-start | bytes 776 | tf_op jit(solution)/shard_map/ppermute | solution.py:13
  43.1 0.2 fusion.6
  43.3 0.6 collective-permute-start.12
  43.8 0.6 fusion.7
  44.4 0.3 fusion.49
  44.7 1.2 %collective-permute-start.10 = (f32[2,4,8]{2,1,0:T(4,128)S(1)}, f32[2,4,8]{2,1,0:T(4,128)S(1)}, u32[]{:S(2)}, u32[]{:S(2)}) collective-permute-start(f32[2,4,8]{2,1,0:T(4,128)S(1)} %get-tuple-element.41), channel_id=1, source_target_pairs={{0,12},{2,14},{4,0},{6,2},{8,4},{10,6},{12,8},{14,10},{1,13},{3,15... | collective-permute-start | bytes 776 | tf_op jit(solution)/shard_map/ppermute | solution.py:13
  45.9 0.2 fusion.8
  46.1 2.0 %collective-permute-start.13 = (f32[2,4,8]{2,1,0:T(4,128)S(1)}, f32[2,4,8]{2,1,0:T(4,128)S(1)}, u32[]{:S(2)}, u32[]{:S(2)}) collective-permute-start(f32[2,4,8]{2,1,0:T(4,128)S(1)} %fusion.8), channel_id=1, source_target_pairs={{0,12},{2,14},{4,0},{6,2},{8,4},{10,6},{12,8},{14,10},{1,13},{3,15... | collective-permute-start | bytes 776 | tf_op jit(solution)/shard_map/ppermute | solution.py:13
  48.1 0.6 fusion.9
  48.6 0.3 fusion.48
  48.9 0.2 fusion.10
  49.1 1.3 %collective-permute-start.14 = (f32[2,4,8]{2,1,0:T(4,128)S(1)}, f32[2,4,8]{2,1,0:T(4,128)S(1)}, u32[]{:S(2)}, u32[]{:S(2)}) collective-permute-start(f32[2,4,8]{2,1,0:T(4,128)S(1)} %fusion.10), channel_id=1, source_target_pairs={{0,10},{2,12},{4,14},{6,0},{8,2},{10,4},{12,6},{14,8},{1,11},{3,13... | collective-permute-start | bytes 776 | tf_op jit(solution)/shard_map/ppermute | solution.py:13
  50.4 0.6 fusion.11
  51.0 1.2 %collective-permute-start.11 = (f32[2,4,8]{2,1,0:T(4,128)S(1)}, f32[2,4,8]{2,1,0:T(4,128)S(1)}, u32[]{:S(2)}, u32[]{:S(2)}) collective-permute-start(f32[2,4,8]{2,1,0:T(4,128)S(1)} %get-tuple-element.39), channel_id=1, source_target_pairs={{0,10},{2,12},{4,14},{6,0},{8,2},{10,4},{12,6},{14,8},{1,11},{3,13... | collective-permute-start | bytes 776 | tf_op jit(solution)/shard_map/ppermute | solution.py:13
  52.2 3.8 %collective-permute-start.2 = (f32[2,4,8,128]{3,2,1,0:T(8,128)S(1)}, f32[2,4,8,128]{3,2,1,0:T(8,128)S(1)}, u32[]{:S(2)}, u32[]{:S(2)}) collective-permute-start(f32[2,4,8,128]{3,2,1,0:T(8,128)S(1)} %fusion.7), channel_id=1, source_target_pairs={{0,14},{2,0},{4,2},{6,4},{8,6},{10,8},{12,10},{14,12},{1,15},{3,1}... | collective-permute-start | bytes 98312 | tf_op jit(solution)/shard_map/ppermute | solution.py:13
  56.1 0.3 collective-permute-start.8
  56.5 0.1 select_reduce_fusion
  56.6 0.4 fusion.16
  57.0 0.5 collective-permute-done.2
  57.6 2.3 %collective-permute-done.5 = f32[2,4,8,128]{3,2,1,0:T(8,128)S(1)} collective-permute-done((f32[2,4,8,128]{3,2,1,0:T(8,128)S(1)}, f32[2,4,8,128]{3,2,1,0:T(8,128)S(1)}, u32[]{:S(2)}, u32[]{:S(2)}) %collective-permute-start.5) | collective-permute-done | bytes 32800 | tf_op jit(solution)/shard_map/ppermute | solution.py:13
  59.9 1.0 %collective-permute-done.8 = f32[2,4,8,128]{3,2,1,0:T(8,128)S(1)} collective-permute-done((f32[2,4,8,128]{3,2,1,0:T(8,128)S(1)}, f32[2,4,8,128]{3,2,1,0:T(8,128)S(1)}, u32[]{:S(2)}, u32[]{:S(2)}) %collective-permute-start.8) | collective-permute-done | bytes 32800 | tf_op jit(solution)/shard_map/ppermute | solution.py:13
  60.9 1.1 %fusion.2 = bf16[2,4,8,128]{3,0,2,1:T(2,128)(2,1)} fusion(f32[8,4,8,128]{3,2,1,0:T(8,128)S(1)} %pad_maximum_fusion, pred[2,8]{1,0:T(4,128)(4,1)S(1)} %compare_and_fusion, f32[2,4,8]{0,2,1:T(8,128)S(1)} %get-tuple-element.17, f32[2,4,128]{2,0,1:T(2,128)S(1)} %copy.63, f32[2,4,8]{0,2,1:T(8,128)S(1)} %get-tuple-element.18, f32[2,4,8]{0,2,1:T(8,128)S(1)} %fusion.23, ...), kind=kOutput, calls=%fused_computation.15 | convolution fusion | flops 820736 | bytes 153360 | tf_op jit(solution)/shard_map/bskg,skgd->bkgd/dot_general | solution.py:108
  (54 shorter events, 0.9 us)
Async XLA Ops:
  3.6 18.1 %collective-permute-start.7 = (s32[2,2]{1,0:T(2,128)S(1)}, s32[2,2]{1,0:T(2,128)S(1)}, u32[]{:S(2)}, u32[]{:S(2)}) collective-permute-start(s32[2,2]{1,0:T(2,128)S(1)} %pad_add_fusion.2), channel_id=1, source_target_pairs={{0,6},{2,8},{4,10},{6,12},{8,14},{10,0},{12,2},{14,4},{1,7},{3,9},... | collective-permute-start | bytes 56 | tf_op jit(solution)/shard_map/ppermute | solution.py:13
  7.7 16.7 %collective-permute-start.4 = (s32[2,2]{1,0:T(2,128)S(1)}, s32[2,2]{1,0:T(2,128)S(1)}, u32[]{:S(2)}, u32[]{:S(2)}) collective-permute-start(s32[2,2]{1,0:T(2,128)S(1)} %pad_add_fusion.1), channel_id=1, source_target_pairs={{0,4},{2,6},{4,8},{6,10},{8,12},{10,14},{12,0},{14,2},{1,5},{3,7},... | collective-permute-start | bytes 56 | tf_op jit(solution)/shard_map/ppermute | solution.py:13
  9.2 15.2 %collective-permute-start.1 = (s32[2,2]{1,0:T(2,128)S(1)}, s32[2,2]{1,0:T(2,128)S(1)}, u32[]{:S(2)}, u32[]{:S(2)}) collective-permute-start(s32[2,2]{1,0:T(2,128)S(1)} %pad_add_fusion), channel_id=1, source_target_pairs={{0,2},{2,4},{4,6},{6,8},{8,10},{10,12},{12,14},{14,0},{1,3},{3,5},... | collective-permute-start | bytes 56 | tf_op jit(solution)/shard_map/ppermute | solution.py:13
  12.1 28.4 %collective-permute-start = (bf16[2,4,8,128]{3,2,1,0:T(8,128)(2,1)S(1)}, bf16[2,4,8,128]{3,2,1,0:T(8,128)(2,1)S(1)}, u32[]{:S(2)}, u32[]{:S(2)}) collective-permute-start(bf16[2,4,8,128]{3,2,1,0:T(8,128)(2,1)S(1)} %gather_fusion.2), channel_id=1, source_target_pairs={{0,2},{2,4},{4,6},{6,8},{8,10},{10,12},{12,14},{14,0},{1,3},{3,5},... | collective-permute-start | bytes 49160 | tf_op jit(solution)/shard_map/ppermute | solution.py:13
  14.2 30.2 %collective-permute-start.3 = (bf16[2,4,8,128]{3,2,1,0:T(8,128)(2,1)S(1)}, bf16[2,4,8,128]{3,2,1,0:T(8,128)(2,1)S(1)}, u32[]{:S(2)}, u32[]{:S(2)}) collective-permute-start(bf16[2,4,8,128]{3,2,1,0:T(8,128)(2,1)S(1)} %gather_fusion.4), channel_id=1, source_target_pairs={{0,4},{2,6},{4,8},{6,10},{8,12},{10,14},{12,0},{14,2},{1,5},{3,7},... | collective-permute-start | bytes 49160 | tf_op jit(solution)/shard_map/ppermute | solution.py:13
  21.7 26.9 %collective-permute-start.6 = (bf16[2,4,8,128]{3,2,1,0:T(8,128)(2,1)S(1)}, bf16[2,4,8,128]{3,2,1,0:T(8,128)(2,1)S(1)}, u32[]{:S(2)}, u32[]{:S(2)}) collective-permute-start(bf16[2,4,8,128]{3,2,1,0:T(8,128)(2,1)S(1)} %gather_fusion.6), channel_id=1, source_target_pairs={{0,6},{2,8},{4,10},{6,12},{8,14},{10,0},{12,2},{14,4},{1,7},{3,9},... | collective-permute-start | bytes 49160 | tf_op jit(solution)/shard_map/ppermute | solution.py:13
  40.8 15.3 %collective-permute-start.9 = (f32[2,4,8]{2,1,0:T(4,128)S(1)}, f32[2,4,8]{2,1,0:T(4,128)S(1)}, u32[]{:S(2)}, u32[]{:S(2)}) collective-permute-start(f32[2,4,8]{2,1,0:T(4,128)S(1)} %get-tuple-element.43), channel_id=1, source_target_pairs={{0,14},{2,0},{4,2},{6,4},{8,6},{10,8},{12,10},{14,12},{1,15},{3,1}... | collective-permute-start | bytes 776 | tf_op jit(solution)/shard_map/ppermute | solution.py:13
  43.3 7.7 %collective-permute-start.12 = (f32[2,4,8]{2,1,0:T(4,128)S(1)}, f32[2,4,8]{2,1,0:T(4,128)S(1)}, u32[]{:S(2)}, u32[]{:S(2)}) collective-permute-start(f32[2,4,8]{2,1,0:T(4,128)S(1)} %fusion.6), channel_id=1, source_target_pairs={{0,14},{2,0},{4,2},{6,4},{8,6},{10,8},{12,10},{14,12},{1,15},{3,1}... | collective-permute-start | bytes 776 | tf_op jit(solution)/shard_map/ppermute | solution.py:13
  44.7 11.7 %collective-permute-start.10 = (f32[2,4,8]{2,1,0:T(4,128)S(1)}, f32[2,4,8]{2,1,0:T(4,128)S(1)}, u32[]{:S(2)}, u32[]{:S(2)}) collective-permute-start(f32[2,4,8]{2,1,0:T(4,128)S(1)} %get-tuple-element.41), channel_id=1, source_target_pairs={{0,12},{2,14},{4,0},{6,2},{8,4},{10,6},{12,8},{14,10},{1,13},{3,15... | collective-permute-start | bytes 776 | tf_op jit(solution)/shard_map/ppermute | solution.py:13
  46.1 6.1 %collective-permute-start.13 = (f32[2,4,8]{2,1,0:T(4,128)S(1)}, f32[2,4,8]{2,1,0:T(4,128)S(1)}, u32[]{:S(2)}, u32[]{:S(2)}) collective-permute-start(f32[2,4,8]{2,1,0:T(4,128)S(1)} %fusion.8), channel_id=1, source_target_pairs={{0,12},{2,14},{4,0},{6,2},{8,4},{10,6},{12,8},{14,10},{1,13},{3,15... | collective-permute-start | bytes 776 | tf_op jit(solution)/shard_map/ppermute | solution.py:13
  49.1 6.9 %collective-permute-start.14 = (f32[2,4,8]{2,1,0:T(4,128)S(1)}, f32[2,4,8]{2,1,0:T(4,128)S(1)}, u32[]{:S(2)}, u32[]{:S(2)}) collective-permute-start(f32[2,4,8]{2,1,0:T(4,128)S(1)} %fusion.10), channel_id=1, source_target_pairs={{0,10},{2,12},{4,14},{6,0},{8,2},{10,4},{12,6},{14,8},{1,11},{3,13... | collective-permute-start | bytes 776 | tf_op jit(solution)/shard_map/ppermute | solution.py:13
  51.0 5.4 %collective-permute-start.11 = (f32[2,4,8]{2,1,0:T(4,128)S(1)}, f32[2,4,8]{2,1,0:T(4,128)S(1)}, u32[]{:S(2)}, u32[]{:S(2)}) collective-permute-start(f32[2,4,8]{2,1,0:T(4,128)S(1)} %get-tuple-element.39), channel_id=1, source_target_pairs={{0,10},{2,12},{4,14},{6,0},{8,2},{10,4},{12,6},{14,8},{1,11},{3,13... | collective-permute-start | bytes 776 | tf_op jit(solution)/shard_map/ppermute | solution.py:13
  52.2 5.4 %collective-permute-start.2 = (f32[2,4,8,128]{3,2,1,0:T(8,128)S(1)}, f32[2,4,8,128]{3,2,1,0:T(8,128)S(1)}, u32[]{:S(2)}, u32[]{:S(2)}) collective-permute-start(f32[2,4,8,128]{3,2,1,0:T(8,128)S(1)} %fusion.7), channel_id=1, source_target_pairs={{0,14},{2,0},{4,2},{6,4},{8,6},{10,8},{12,10},{14,12},{1,15},{3,1}... | collective-permute-start | bytes 98312 | tf_op jit(solution)/shard_map/ppermute | solution.py:13
  56.0 3.9 %collective-permute-start.5 = (f32[2,4,8,128]{3,2,1,0:T(8,128)S(1)}, f32[2,4,8,128]{3,2,1,0:T(8,128)S(1)}, u32[]{:S(2)}, u32[]{:S(2)}) collective-permute-start(f32[2,4,8,128]{3,2,1,0:T(8,128)S(1)} %fusion.9), channel_id=1, source_target_pairs={{0,12},{2,14},{4,0},{6,2},{8,4},{10,6},{12,8},{14,10},{1,13},{3,15... | collective-permute-start | bytes 98312 | tf_op jit(solution)/shard_map/ppermute | solution.py:13
  56.1 4.8 %collective-permute-start.8 = (f32[2,4,8,128]{3,2,1,0:T(8,128)S(1)}, f32[2,4,8,128]{3,2,1,0:T(8,128)S(1)}, u32[]{:S(2)}, u32[]{:S(2)}) collective-permute-start(f32[2,4,8,128]{3,2,1,0:T(8,128)S(1)} %fusion.11), channel_id=1, source_target_pairs={{0,10},{2,12},{4,14},{6,0},{8,2},{10,4},{12,6},{14,8},{1,11},{3,13... | collective-permute-start | bytes 98312 | tf_op jit(solution)/shard_map/ppermute | solution.py:13
where the time goes:
time: 62.6 us; the launch traced here: 62 us
  local copies, waits for them, and re-layouts  24.3 us (39%)
  starting transfers between devices  24.3 us (39%)
  matrix products  5.57 us (9%)
  waiting for transfers between devices  3.87 us (6%)
  other arithmetic  3.58 us (6%)
    ppermute x15, starting transfers between devices, shifted(): return lax.ppermute(value, axis, pairs)  24.3 us
    gather x4, local copies, waits for them, and re-layouts, body(): served = kv_pages[incoming[0]]  11.2 us
    slice x8, local copies, waits for them, and re-layouts, page_partial(): keys = served[:, 0].reshape(slots, length, kv_count, width // kv_count)  5.2 us
    ppermute x15, waiting for transfers between devices, shifted(): return lax.ppermute(value, axis, pairs)  3.87 us
    slice x4, local copies, waits for them, and re-layouts, page_partial(): values = served[:, 1].reshape(slots, length, kv_count, width // kv_count)  2.9 us
    gather x4, local copies, waits for them, and re-layouts, body(): query_rows = query_head_count[seq_slot]  2.23 us
    dot_general x4, matrix products, page_partial(): jnp.einsum('ckgp,cpkd->ckgd', weights, values.astype(jnp.float32), precis...  2.22 us
  transfers between devices with their start and end apart: 15, of which 3 were waited for; matrix products, arithmetic and copies ran while one was open for 46% of the time, Pallas kernels for 0%

commit v1 on v0

v1 whole, which is shorter than its diff:
```python
import functools

import jax
import jax.numpy as jnp
from jax import lax
from jax.experimental import pallas as pl
from jax.experimental.pallas import tpu as pltpu
from jax.sharding import PartitionSpec as P

HEAD_DIM = 128
REACH = 4
MASKED = -1e30
FLOOR = -1e29
MESH = pl.DeviceIdType.MESH


def plan(places, owners, lengths, slot, me, seq_count, most_pages, capacity):
    pages = [jnp.int32(0)] * capacity
    seqs = [jnp.int32(-1)] * capacity
    rank = jnp.int32(0)
    for s in range(seq_count):
        length = lengths[slot, 0, s]
        for j in range(most_pages):
            hit = jnp.logical_and(j < length, owners[slot, s, j] == me)
            place = places[slot, s, j]
            for c in range(capacity):
                mine = jnp.logical_and(hit, rank == c)
                pages[c] = jnp.where(mine, place, pages[c])
                seqs[c] = jnp.where(mine, s, seqs[c])
            rank = rank + hit.astype(jnp.int32)
    return pages, seqs


def kernel(
    n, seq_count, most_pages, capacity, kv_count, rows, order, scale,
    q_ref, fresh_ref, kv_ref, places_ref, owners_ref, lengths_ref, out_ref,
    key_shelf, value_shelf, q_in, fresh, places, owners, lengths, part_out, part_in,
    shelf_sem, local_sem, ask_send, ask_recv, back_send, back_recv,
):
    me = lax.axis_index("store")

    def at(steps):
        return {"store": lax.rem(me + steps + n, n)}

    loads = [
        pltpu.make_async_copy(kv_ref.at[:, i], half, shelf_sem.at[i])
        for i, half in enumerate((key_shelf, value_shelf))
    ]
    asked = ((q_ref, q_in), (places_ref, places), (owners_ref, owners), (lengths_ref, lengths))
    locals_ = [
        pltpu.make_async_copy(source, target.at[0], local_sem.at[i])
        for i, (source, target) in enumerate(asked)
    ]
    locals_.append(pltpu.make_async_copy(fresh_ref, fresh, local_sem.at[len(asked)]))

    barrier = pltpu.get_barrier_semaphore()
    for d in range(1, REACH):
        for sign in (1, -1):
            pl.semaphore_signal(barrier, inc=1, device_id=at(sign * d), device_id_type=MESH)
    for copy in locals_ + loads:
        copy.start()
    pl.semaphore_wait(barrier, 2 * (REACH - 1))

    asks = {}
    for d in reversed(order):
        asks[d] = [
            pltpu.make_async_remote_copy(
                src_ref=source,
                dst_ref=target.at[d],
                send_sem=ask_send.at[i, d - 1],
                recv_sem=ask_recv.at[i, d - 1],
                device_id=at(d),
                device_id_type=MESH,
            )
            for i, (source, target) in enumerate(asked)
        ]
        for copy in asks[d]:
            copy.start()

    turn = lax.rem(lax.broadcasted_iota(jnp.int32, (rows, 1), 0), seq_count)
    lane = lax.broadcasted_iota(jnp.int32, (rows, HEAD_DIM), 1)

    def partial_of(slot, wait_values=None):
        pages, seqs = plan(places, owners, lengths, slot, me, seq_count, most_pages, capacity)
        bias = [jnp.where(turn == seq, jnp.float32(0.0), jnp.float32(MASKED)) for seq in seqs]
        scores = []
        for k in range(kv_count):
            qk = q_in[slot, k * rows : (k + 1) * rows, :]
            row = []
            for c in range(capacity):
                keys = key_shelf[pages[c], :, k * HEAD_DIM : (k + 1) * HEAD_DIM]
                dots = lax.dot_general(
                    qk, keys, (((1,), (1,)), ((), ())), preferred_element_type=jnp.float32
                )
                row.append(dots * scale + bias[c])
            scores.append(row)
        if wait_values is not None:
            wait_values()
        peaks, totals, sums = [], [], []
        for k in range(kv_count):
            peak = functools.reduce(jnp.maximum, [jnp.max(s, axis=1, keepdims=True) for s in scores[k]])
            peak = jnp.maximum(peak, jnp.float32(FLOOR))
            total = jnp.float32(0.0)
            summed = jnp.float32(0.0)
            for c in range(capacity):
                w = jnp.exp(scores[k][c] - peak)
                total = total + jnp.sum(w, axis=1, keepdims=True)
                high = w.astype(jnp.bfloat16)
                low = (w - high.astype(jnp.float32)).astype(jnp.bfloat16)
                values = value_shelf[pages[c], :, k * HEAD_DIM : (k + 1) * HEAD_DIM]
                summed = summed + jnp.dot(
                    jnp.concatenate([high, low], axis=0), values, preferred_element_type=jnp.float32
                )
            peaks.append(peak)
            totals.append(total)
            sums.append(summed[:rows] + summed[rows:])
        return peaks, totals, sums

    for copy in locals_:
        copy.wait()
    loads[0].wait()
    peaks, totals, sums = partial_of(0, loads[1].wait)
    for k in range(kv_count):
        qk = q_in[0, k * rows : (k + 1) * rows, :].astype(jnp.float32)
        cut = slice(k * HEAD_DIM, (k + 1) * HEAD_DIM)
        key = fresh[0, 0:1, cut].astype(jnp.float32)
        value = fresh[0, 1:2, cut].astype(jnp.float32)
        for s in range(1, seq_count):
            key = jnp.where(turn == s, fresh[s, 0:1, cut].astype(jnp.float32), key)
            value = jnp.where(turn == s, fresh[s, 1:2, cut].astype(jnp.float32), value)
        own = jnp.sum(qk * key, axis=1, keepdims=True) * scale
        peak = jnp.maximum(peaks[k], own)
        factor = jnp.exp(peaks[k] - peak)
        weight = jnp.exp(own - peak)
        peaks[k] = peak
        totals[k] = totals[k] * factor + weight
        sums[k] = sums[k] * factor + weight * value

    backs = {}
    for d in order:
        for copy in asks[d]:
            copy.wait_recv()
        theirs = partial_of(d)
        stats = jnp.zeros((rows, HEAD_DIM), jnp.float32)
        for k in range(kv_count):
            part_out[d - 1, k * rows : (k + 1) * rows, :] = theirs[2][k]
            stats = jnp.where(lane == 2 * k, theirs[0][k], stats)
            stats = jnp.where(lane == 2 * k + 1, theirs[1][k], stats)
        part_out[d - 1, kv_count * rows :, :] = stats
        backs[d] = pltpu.make_async_remote_copy(
            src_ref=part_out.at[d - 1],
            dst_ref=part_in.at[d - 1],
            send_sem=back_send.at[d - 1],
            recv_sem=back_recv.at[d - 1],
            device_id=at(-d),
            device_id_type=MESH,
        )
        backs[d].start()

    for d in order:
        backs[d].wait_recv()
    for k in range(kv_count):
        part_peaks = [part_in[d - 1, kv_count * rows :, 2 * k : 2 * k + 1] for d in order]
        part_totals = [part_in[d - 1, kv_count * rows :, 2 * k + 1 : 2 * k + 2] for d in order]
        highest = functools.reduce(jnp.maximum, part_peaks, peaks[k])
        factor = jnp.exp(peaks[k] - highest)
        total = totals[k] * factor
        summed = sums[k] * factor
        for i, d in enumerate(order):
            factor = jnp.exp(part_peaks[i] - highest)
            total = total + part_totals[i] * factor
            summed = summed + part_in[d - 1, k * rows : (k + 1) * rows, :] * factor
        out_ref[k * rows : (k + 1) * rows, :] = (summed / total).astype(out_ref.dtype)
    for d in order:
        for copy in asks[d]:
            copy.wait_send()
        backs[d].wait_send()


def body(queries, new_kv, kv_pages, page_index, page_owner, seq_pages):
    n = lax.axis_size("store")
    seq_count, most_pages = page_index.shape
    kv_count = new_kv.shape[2] // HEAD_DIM
    heads = queries.shape[1] // HEAD_DIM
    rows = heads // kv_count * seq_count
    all_rows = heads * seq_count
    capacity = seq_count * most_pages // REACH
    q = queries.reshape(seq_count, heads, HEAD_DIM).transpose(1, 0, 2).reshape(all_rows, HEAD_DIM)
    away = REACH - 1
    half = kv_pages.shape[:1] + kv_pages.shape[2:]
    order = (2, 1) + tuple(range(3, REACH))
    out = pl.pallas_call(
        functools.partial(
            kernel, n, seq_count, most_pages, capacity, kv_count, rows, order, HEAD_DIM ** (-0.5)
        ),
        out_shape=jax.ShapeDtypeStruct((all_rows, HEAD_DIM), jnp.bfloat16),
        in_specs=[pl.BlockSpec(memory_space=pl.ANY)] * 6,
        out_specs=pl.BlockSpec(memory_space=pltpu.VMEM),
        scratch_shapes=[
            pltpu.VMEM(half, kv_pages.dtype),
            pltpu.VMEM(half, kv_pages.dtype),
            pltpu.VMEM((REACH, all_rows, HEAD_DIM), q.dtype),
            pltpu.VMEM(new_kv.shape, new_kv.dtype),
            pltpu.SMEM((REACH, seq_count, most_pages), jnp.int32),
            pltpu.SMEM((REACH, seq_count, most_pages), jnp.int32),
            pltpu.SMEM((REACH, 1, seq_count), jnp.int32),
            pltpu.VMEM((away, all_rows + rows, HEAD_DIM), jnp.float32),
            pltpu.VMEM((away, all_rows + rows, HEAD_DIM), jnp.float32),
            pltpu.SemaphoreType.DMA((2,)),
            pltpu.SemaphoreType.DMA((5,)),
            pltpu.SemaphoreType.DMA((4, away)),
            pltpu.SemaphoreType.DMA((4, away)),
            pltpu.SemaphoreType.DMA((away,)),
            pltpu.SemaphoreType.DMA((away,)),
        ],
        compiler_params=pltpu.CompilerParams(collective_id=0, has_side_effects=True),
    )(q, new_kv, kv_pages, page_index, page_owner, seq_pages.reshape(1, seq_count))
    out = out.reshape(heads, seq_count, HEAD_DIM).transpose(1, 0, 2)
    return out.reshape(seq_count, heads * HEAD_DIM)


def solution(mesh):
    in_specs = (
        P(("groups", "store"), "tensor"),
        P(("groups", "store"), None, "tensor"),
        P(("groups", "store"), None, None, "tensor"),
        P(("groups", "store"), None),
        P(("groups", "store"), None),
        P(("groups", "store")),
    )
    out_specs = P(("groups", "store"), "tensor")
    return jax.shard_map(body, mesh=mesh, in_specs=in_specs, out_specs=out_specs, check_vma=False)
```

time: 62.6 us -> 17.2 us (0.27)
  starting transfers between devices: 24.3 us -> 0 us
  local copies, waits for them, and re-layouts: 24.3 us -> 1.34 us
  Pallas kernels: 0 us -> 15.6 us
  matrix products: 5.57 us -> 0 us
  waiting for transfers between devices: 3.87 us -> 0 us
  other arithmetic: 3.58 us -> 0 us
    ppermute x15 -> x0, starting transfers between devices: 24.3 us -> none  [shifted(): return lax.ppermute(value, axis, pairs)]
    pallas_call x0 -> x1, Pallas kernels: none -> 15.6 us  [body(): pl.pallas_call(functools.partial(kernel, n, seq_count, most_pages, capaci...]
    gather x8 -> x0, local copies, waits for them, and re-layouts: 13.4 us -> none  [the longest x4 11.2 us: body(): served = kv_pages[incoming[0]]]
    slice x12 -> x0, local copies, waits for them, and re-layouts: 8.09 us -> none  [the longest x8 5.2 us: page_partial(): keys = served[:, 0].reshape(slots, length, kv_count, width // kv_count)]
    dot_general x11 -> x0, matrix products: 5.57 us -> none  [the longest x4 2.22 us: page_partial(): jnp.einsum('ckgp,cpkd->ckgd', weights, values.astype(jnp.float32), precis...]
    ppermute x15 -> x0, waiting for transfers between devices: 3.87 us -> none  [shifted(): return lax.ppermute(value, axis, pairs)]
    reduce_sum x5 -> x0, other arithmetic: 0.99 us -> none  [the longest x4 0.69 us: page_partial(): total = jnp.sum(weights, axis=-1)]
    mul x1 -> x0, local copies, waits for them, and re-layouts: 0.76 us -> none  [slot_plan(): wanted = jnp.sum(picker * places_table.reshape(-1)[None, :], axis=1)]
  transfers between devices with their start and end apart: 15 -> 0, of which waited for: 3 -> 0; matrix products, arithmetic and copies ran while one was open for 46% -> 0% of each run, Pallas kernels for 0% -> 0%
where the time goes in v1:
time: 17.2 us; the launch traced here: 16.9 us
  Pallas kernels  15.6 us (91%)
  local copies, waits for them, and re-layouts  1.34 us (8%)
    pallas_call x1, Pallas kernels, body(): pl.pallas_call(functools.partial(kernel, n, seq_count, most_pages, capaci...  15.6 us
    unnamed x1, local copies, waits for them, and re-layouts  1.34 us

profile of v1, /device:TPU:0, one launch (start us, length us, event | category | flops | bytes accessed | tf_op | source)
XLA Modules:
  0.0 16.9 jit_solution(16748516070790304841)
XLA Ops:
  0.0 15.6 %shard_map.64 = bf16[64,128]{1,0:T(8,128)(2,1)} custom-call(bf16[64,128]{1,0:T(8,128)(2,1)} %bitcast.12, bf16[2,2,512]{2,1,0:T(2,128)(2,1)} %fresh_ref.1, bf16[8,2,256,512]{3,2,1,0:T(8,128)(2,1)} %kv_ref.1, s32[2,4]{1,0:T(2,128)} %places_ref.1, s32[2,4]{1,0:T(2,128)} %owners_ref.1, s32[1,2]{1,0:T(1,128)} %bitcast.13), custom_call_target="tpu_custom_call" | custom-call | tf_op jit(solution)/shard_map/pallas_call | solution.py:192
  15.6 1.3 %copy.10 = bf16[2,4096]{1,0:T(2,128)(2,1)} copy(bf16[2,4096]{1,0:T(2,128)(2,1)} %bitcast.11) | data formatting | bytes 32768

commit v2 on v1

--- a/solution.py
+++ b/solution.py
@@ -59,13 +59,15 @@
             pl.semaphore_signal(barrier, inc=1, device_id=at(sign * d), device_id_type=MESH)
     for copy in locals_ + loads:
         copy.start()
+    for copy in locals_:
+        copy.wait()
     pl.semaphore_wait(barrier, 2 * (REACH - 1))
 
     asks = {}
     for d in reversed(order):
         asks[d] = [
             pltpu.make_async_remote_copy(
-                src_ref=source,
+                src_ref=target.at[0],
                 dst_ref=target.at[d],
                 send_sem=ask_send.at[i, d - 1],
                 recv_sem=ask_recv.at[i, d - 1],
@@ -116,8 +118,6 @@
             sums.append(summed[:rows] + summed[rows:])
         return peaks, totals, sums
 
-    for copy in locals_:
-        copy.wait()
     loads[0].wait()
     peaks, totals, sums = partial_of(0, loads[1].wait)
     for k in range(kv_count):
@@ -188,12 +188,12 @@
     q = queries.reshape(seq_count, heads, HEAD_DIM).transpose(1, 0, 2).reshape(all_rows, HEAD_DIM)
     away = REACH - 1
     half = kv_pages.shape[:1] + kv_pages.shape[2:]
-    order = (2, 1) + tuple(range(3, REACH))
+    order = (1, 2, 3)
     out = pl.pallas_call(
         functools.partial(
             kernel, n, seq_count, most_pages, capacity, kv_count, rows, order, HEAD_DIM ** (-0.5)
         ),
-        out_shape=jax.ShapeDtypeStruct((all_rows, HEAD_DIM), jnp.bfloat16),
+        out_shape=pltpu.VMEM((all_rows, HEAD_DIM), jnp.bfloat16),
         in_specs=[pl.BlockSpec(memory_space=pl.ANY)] * 6,
         out_specs=pl.BlockSpec(memory_space=pltpu.VMEM),
         scratch_shapes=[

time: 17.2 us -> 15.3 us (0.89)
  Pallas kernels: 15.6 us -> 14.5 us
  local copies, waits for them, and re-layouts: 1.34 us -> 0.61 us
    pallas_call x1, Pallas kernels: 15.6 us -> 14.5 us  [body(): pl.pallas_call(functools.partial(kernel, n, seq_count, most_pages, capaci...]
    unnamed x1, local copies, waits for them, and re-layouts: 1.34 us -> 0.61 us
where the time goes in v2:
time: 15.3 us; the launch traced here: 15.1 us
  Pallas kernels  14.5 us (95%)
  local copies, waits for them, and re-layouts  0.61 us (4%)
    pallas_call x1, Pallas kernels, body(): pl.pallas_call(functools.partial(kernel, n, seq_count, most_pages, capaci...  14.5 us
    unnamed x1, local copies, waits for them, and re-layouts  0.61 us

profile of v2, /device:TPU:0, one launch (start us, length us, event | category | flops | bytes accessed | tf_op | source)
XLA Modules:
  0.0 15.1 jit_solution(12925031803834877087)
XLA Ops:
  0.0 14.5 %shard_map.64 = bf16[64,128]{1,0:T(8,128)(2,1)S(1)} custom-call(bf16[64,128]{1,0:T(8,128)(2,1)} %bitcast.12, bf16[2,2,512]{2,1,0:T(2,128)(2,1)} %fresh_ref.1, bf16[8,2,256,512]{3,2,1,0:T(8,128)(2,1)} %kv_ref.1, s32[2,4]{1,0:T(2,128)} %places_ref.1, s32[2,4]{1,0:T(2,128)} %owners_ref.1, s32[1,2]{1,0:T(1,128)} %bitcast.13), custom_call_target="tpu_custom_call" | custom-call | tf_op jit(solution)/shard_map/pallas_call | solution.py:192
  14.5 0.6 %copy.10 = bf16[2,4096]{1,0:T(2,128)(2,1)} copy(bf16[2,4096]{1,0:T(2,128)(2,1)S(1)} %bitcast.11) | data formatting | bytes 32768

commit v3 on v2

--- a/solution.py
+++ b/solution.py
@@ -14,27 +14,26 @@
 MESH = pl.DeviceIdType.MESH
 
 
-def plan(places, owners, lengths, slot, me, seq_count, most_pages, capacity):
+def plan(places, owners, lengths, owner, seq_count, most_pages, capacity):
     pages = [jnp.int32(0)] * capacity
     seqs = [jnp.int32(-1)] * capacity
     rank = jnp.int32(0)
     for s in range(seq_count):
-        length = lengths[slot, 0, s]
+        length = lengths[0, s]
         for j in range(most_pages):
-            hit = jnp.logical_and(j < length, owners[slot, s, j] == me)
-            place = places[slot, s, j]
+            hit = jnp.logical_and(j < length, owners[s, j] == owner)
             for c in range(capacity):
                 mine = jnp.logical_and(hit, rank == c)
-                pages[c] = jnp.where(mine, place, pages[c])
+                pages[c] = jnp.where(mine, places[s, j], pages[c])
                 seqs[c] = jnp.where(mine, s, seqs[c])
             rank = rank + hit.astype(jnp.int32)
-    return pages, seqs
+    return pages + seqs
 
 
 def kernel(
     n, seq_count, most_pages, capacity, kv_count, rows, order, scale,
     q_ref, fresh_ref, kv_ref, places_ref, owners_ref, lengths_ref, out_ref,
-    key_shelf, value_shelf, q_in, fresh, places, owners, lengths, part_out, part_in,
+    key_shelf, value_shelf, q_in, fresh, places, owners, lengths, wants, asked, part_out, part_in,
     shelf_sem, local_sem, ask_send, ask_recv, back_send, back_recv,
 ):
     me = lax.axis_index("store")
@@ -46,35 +45,45 @@
         pltpu.make_async_copy(kv_ref.at[:, i], half, shelf_sem.at[i])
         for i, half in enumerate((key_shelf, value_shelf))
     ]
-    asked = ((q_ref, q_in), (places_ref, places), (owners_ref, owners), (lengths_ref, lengths))
     locals_ = [
-        pltpu.make_async_copy(source, target.at[0], local_sem.at[i])
-        for i, (source, target) in enumerate(asked)
+        pltpu.make_async_copy(source, target, local_sem.at[i])
+        for i, (source, target) in enumerate(
+            (
+                (places_ref, places),
+                (owners_ref, owners),
+                (lengths_ref, lengths),
+                (q_ref, q_in.at[0]),
+                (fresh_ref, fresh),
+            )
+        )
     ]
-    locals_.append(pltpu.make_async_copy(fresh_ref, fresh, local_sem.at[len(asked)]))
 
     barrier = pltpu.get_barrier_semaphore()
     for d in range(1, REACH):
-        for sign in (1, -1):
-            pl.semaphore_signal(barrier, inc=1, device_id=at(sign * d), device_id_type=MESH)
+        pl.semaphore_signal(barrier, inc=1, device_id=at(-d), device_id_type=MESH)
     for copy in locals_ + loads:
         copy.start()
     for copy in locals_:
         copy.wait()
-    pl.semaphore_wait(barrier, 2 * (REACH - 1))
+    for d in range(REACH):
+        owner = lax.rem(me + d, n)
+        wanted = plan(places, owners, lengths, owner, seq_count, most_pages, capacity)
+        for i, word in enumerate(wanted):
+            wants[d, 0, i] = word
+    pl.semaphore_wait(barrier, REACH - 1)
 
     asks = {}
-    for d in reversed(order):
+    for d in order:
         asks[d] = [
             pltpu.make_async_remote_copy(
-                src_ref=target.at[0],
+                src_ref=source,
                 dst_ref=target.at[d],
                 send_sem=ask_send.at[i, d - 1],
                 recv_sem=ask_recv.at[i, d - 1],
                 device_id=at(d),
                 device_id_type=MESH,
             )
-            for i, (source, target) in enumerate(asked)
+            for i, (source, target) in enumerate(((wants.at[d], asked), (q_in.at[0], q_in)))
         ]
         for copy in asks[d]:
             copy.start()
@@ -82,8 +91,9 @@
     turn = lax.rem(lax.broadcasted_iota(jnp.int32, (rows, 1), 0), seq_count)
     lane = lax.broadcasted_iota(jnp.int32, (rows, HEAD_DIM), 1)
 
-    def partial_of(slot, wait_values=None):
-        pages, seqs = plan(places, owners, lengths, slot, me, seq_count, most_pages, capacity)
+    def partial_of(words, slot, wait_values=None):
+        pages = [words[slot, 0, c] for c in range(capacity)]
+        seqs = [words[slot, 0, capacity + c] for c in range(capacity)]
         bias = [jnp.where(turn == seq, jnp.float32(0.0), jnp.float32(MASKED)) for seq in seqs]
         scores = []
         for k in range(kv_count):
@@ -119,7 +129,7 @@
         return peaks, totals, sums
 
     loads[0].wait()
-    peaks, totals, sums = partial_of(0, loads[1].wait)
+    peaks, totals, sums = partial_of(wants, 0, loads[1].wait)
     for k in range(kv_count):
         qk = q_in[0, k * rows : (k + 1) * rows, :].astype(jnp.float32)
         cut = slice(k * HEAD_DIM, (k + 1) * HEAD_DIM)
@@ -140,7 +150,7 @@
     for d in order:
         for copy in asks[d]:
             copy.wait_recv()
-        theirs = partial_of(d)
+        theirs = partial_of(asked, d)
         stats = jnp.zeros((rows, HEAD_DIM), jnp.float32)
         for k in range(kv_count):
             part_out[d - 1, k * rows : (k + 1) * rows, :] = theirs[2][k]
@@ -159,18 +169,17 @@
 
     for d in order:
         backs[d].wait_recv()
+        for k in range(kv_count):
+            part_peak = part_in[d - 1, kv_count * rows :, 2 * k : 2 * k + 1]
+            part_total = part_in[d - 1, kv_count * rows :, 2 * k + 1 : 2 * k + 2]
+            peak = jnp.maximum(peaks[k], part_peak)
+            factor = jnp.exp(peaks[k] - peak)
+            part_factor = jnp.exp(part_peak - peak)
+            peaks[k] = peak
+            totals[k] = totals[k] * factor + part_total * part_factor
+            sums[k] = sums[k] * factor + part_in[d - 1, k * rows : (k + 1) * rows, :] * part_factor
     for k in range(kv_count):
-        part_peaks = [part_in[d - 1, kv_count * rows :, 2 * k : 2 * k + 1] for d in order]
-        part_totals = [part_in[d - 1, kv_count * rows :, 2 * k + 1 : 2 * k + 2] for d in order]
-        highest = functools.reduce(jnp.maximum, part_peaks, peaks[k])
-        factor = jnp.exp(peaks[k] - highest)
-        total = totals[k] * factor
-        summed = sums[k] * factor
-        for i, d in enumerate(order):
-            factor = jnp.exp(part_peaks[i] - highest)
-            total = total + part_totals[i] * factor
-            summed = summed + part_in[d - 1, k * rows : (k + 1) * rows, :] * factor
-        out_ref[k * rows : (k + 1) * rows, :] = (summed / total).astype(out_ref.dtype)
+        out_ref[k * rows : (k + 1) * rows, :] = (sums[k] / totals[k]).astype(out_ref.dtype)
     for d in order:
         for copy in asks[d]:
             copy.wait_send()
@@ -201,15 +210,17 @@
             pltpu.VMEM(half, kv_pages.dtype),
             pltpu.VMEM((REACH, all_rows, HEAD_DIM), q.dtype),
             pltpu.VMEM(new_kv.shape, new_kv.dtype),
-            pltpu.SMEM((REACH, seq_count, most_pages), jnp.int32),
-            pltpu.SMEM((REACH, seq_count, most_pages), jnp.int32),
-            pltpu.SMEM((REACH, 1, seq_count), jnp.int32),
+            pltpu.SMEM(page_index.shape, jnp.int32),
+            pltpu.SMEM(page_owner.shape, jnp.int32),
+            pltpu.SMEM((1, seq_count), jnp.int32),
+            pltpu.SMEM((REACH, 1, 2 * capacity), jnp.int32),
+            pltpu.SMEM((REACH, 1, 2 * capacity), jnp.int32),
             pltpu.VMEM((away, all_rows + rows, HEAD_DIM), jnp.float32),
             pltpu.VMEM((away, all_rows + rows, HEAD_DIM), jnp.float32),
             pltpu.SemaphoreType.DMA((2,)),
             pltpu.SemaphoreType.DMA((5,)),
-            pltpu.SemaphoreType.DMA((4, away)),
-            pltpu.SemaphoreType.DMA((4, away)),
+            pltpu.SemaphoreType.DMA((2, away)),
+            pltpu.SemaphoreType.DMA((2, away)),
             pltpu.SemaphoreType.DMA((away,)),
             pltpu.SemaphoreType.DMA((away,)),
         ],

time: 15.3 us -> 13.7 us (0.90)
  Pallas kernels: 14.5 us -> 12.9 us
    pallas_call x1, Pallas kernels: 14.5 us -> 12.9 us  [body(): pl.pallas_call(functools.partial(kernel, n, seq_count, most_pages, capaci...]
where the time goes in v3:
time: 13.7 us; the launch traced here: 13.5 us
  Pallas kernels  12.9 us (94%)
  local copies, waits for them, and re-layouts  0.61 us (4%)
    pallas_call x1, Pallas kernels, body(): pl.pallas_call(functools.partial(kernel, n, seq_count, most_pages, capaci...  12.9 us
    unnamed x1, local copies, waits for them, and re-layouts  0.61 us

profile of v3, /device:TPU:0, one launch (start us, length us, event | category | flops | bytes accessed | tf_op | source)
XLA Modules:
  0.0 13.5 jit_solution(17737131768693422313)
XLA Ops:
  0.0 12.9 %shard_map.64 = bf16[64,128]{1,0:T(8,128)(2,1)S(1)} custom-call(bf16[64,128]{1,0:T(8,128)(2,1)} %bitcast.12, bf16[2,2,512]{2,1,0:T(2,128)(2,1)} %fresh_ref.1, bf16[8,2,256,512]{3,2,1,0:T(8,128)(2,1)} %kv_ref.1, s32[2,4]{1,0:T(2,128)} %places_ref.1, s32[2,4]{1,0:T(2,128)} %owners_ref.1, s32[1,2]{1,0:T(1,128)} %bitcast.13), custom_call_target="tpu_custom_call" | custom-call | tf_op jit(solution)/shard_map/pallas_call | solution.py:201
  12.9 0.6 %copy.10 = bf16[2,4096]{1,0:T(2,128)(2,1)} copy(bf16[2,4096]{1,0:T(2,128)(2,1)S(1)} %bitcast.11) | data formatting | bytes 32768

commit v4 on v3

--- a/solution.py
+++ b/solution.py
@@ -33,7 +33,7 @@
 def kernel(
     n, seq_count, most_pages, capacity, kv_count, rows, order, scale,
     q_ref, fresh_ref, kv_ref, places_ref, owners_ref, lengths_ref, out_ref,
-    key_shelf, value_shelf, q_in, fresh, places, owners, lengths, wants, asked, part_out, part_in,
+    key_shelf, value_shelf, turned, q_in, fresh, places, owners, lengths, wants, asked, part_out, part_in,
     shelf_sem, local_sem, ask_send, ask_recv, back_send, back_recv,
 ):
     me = lax.axis_index("store")
@@ -100,9 +100,10 @@
             qk = q_in[slot, k * rows : (k + 1) * rows, :]
             row = []
             for c in range(capacity):
-                keys = key_shelf[pages[c], :, k * HEAD_DIM : (k + 1) * HEAD_DIM]
+                cut = slice(k * HEAD_DIM, (k + 1) * HEAD_DIM)
+                keys, inner = (key_shelf[pages[c], :, cut], 1) if slot == 0 else (turned[pages[c], cut, :], 0)
                 dots = lax.dot_general(
-                    qk, keys, (((1,), (1,)), ((), ())), preferred_element_type=jnp.float32
+                    qk, keys, (((1,), (inner,)), ((), ())), preferred_element_type=jnp.float32
                 )
                 row.append(dots * scale + bias[c])
             scores.append(row)
@@ -145,6 +146,12 @@
         peaks[k] = peak
         totals[k] = totals[k] * factor + weight
         sums[k] = sums[k] * factor + weight * value
+
+    @pl.loop(0, key_shelf.shape[0])
+    def _(page):
+        for k in range(kv_count):
+            cut = slice(k * HEAD_DIM, (k + 1) * HEAD_DIM)
+            turned[page, cut, :] = key_shelf[page, :, cut].T
 
     backs = {}
     for d in order:
@@ -208,6 +215,7 @@
         scratch_shapes=[
             pltpu.VMEM(half, kv_pages.dtype),
             pltpu.VMEM(half, kv_pages.dtype),
+            pltpu.VMEM((half[0], half[2], half[1]), kv_pages.dtype),
             pltpu.VMEM((REACH, all_rows, HEAD_DIM), q.dtype),
             pltpu.VMEM(new_kv.shape, new_kv.dtype),
             pltpu.SMEM(page_index.shape, jnp.int32),

time: 13.7 us -> 13.4 us (0.978)
  Pallas kernels: 12.9 us -> 12.7 us
    pallas_call x1, Pallas kernels: 12.9 us -> 12.7 us  [body(): pl.pallas_call(functools.partial(kernel, n, seq_count, most_pages, capaci...]
where the time goes in v4:
time: 13.4 us; the launch traced here: 13.3 us
  Pallas kernels  12.7 us (95%)
  local copies, waits for them, and re-layouts  0.61 us (5%)
    pallas_call x1, Pallas kernels, body(): pl.pallas_call(functools.partial(kernel, n, seq_count, most_pages, capaci...  12.7 us
    unnamed x1, local copies, waits for them, and re-layouts  0.61 us

profile of v4, /device:TPU:0, one launch (start us, length us, event | category | flops | bytes accessed | tf_op | source)
XLA Modules:
  0.0 13.3 jit_solution(11418715646117785571)
XLA Ops:
  0.0 12.7 %shard_map.64 = bf16[64,128]{1,0:T(8,128)(2,1)S(1)} custom-call(bf16[64,128]{1,0:T(8,128)(2,1)} %bitcast.12, bf16[2,2,512]{2,1,0:T(2,128)(2,1)} %fresh_ref.1, bf16[8,2,256,512]{3,2,1,0:T(8,128)(2,1)} %kv_ref.1, s32[2,4]{1,0:T(2,128)} %places_ref.1, s32[2,4]{1,0:T(2,128)} %owners_ref.1, s32[1,2]{1,0:T(1,128)} %bitcast.13), custom_call_target="tpu_custom_call" | custom-call | tf_op jit(solution)/shard_map/pallas_call | solution.py:208
  12.7 0.6 %copy.10 = bf16[2,4096]{1,0:T(2,128)(2,1)} copy(bf16[2,4096]{1,0:T(2,128)(2,1)S(1)} %bitcast.11) | data formatting | bytes 32768

commit v5 on v4

--- a/solution.py
+++ b/solution.py
@@ -160,37 +160,47 @@
         theirs = partial_of(asked, d)
         stats = jnp.zeros((rows, HEAD_DIM), jnp.float32)
         for k in range(kv_count):
-            part_out[d - 1, k * rows : (k + 1) * rows, :] = theirs[2][k]
             stats = jnp.where(lane == 2 * k, theirs[0][k], stats)
             stats = jnp.where(lane == 2 * k + 1, theirs[1][k], stats)
-        part_out[d - 1, kv_count * rows :, :] = stats
-        backs[d] = pltpu.make_async_remote_copy(
-            src_ref=part_out.at[d - 1],
-            dst_ref=part_in.at[d - 1],
-            send_sem=back_send.at[d - 1],
-            recv_sem=back_recv.at[d - 1],
-            device_id=at(-d),
-            device_id_type=MESH,
-        )
-        backs[d].start()
-
-    for d in order:
-        backs[d].wait_recv()
-        for k in range(kv_count):
-            part_peak = part_in[d - 1, kv_count * rows :, 2 * k : 2 * k + 1]
-            part_total = part_in[d - 1, kv_count * rows :, 2 * k + 1 : 2 * k + 2]
+        part_out[d - 1, :rows, :] = stats
+        cuts = (0, (1 + kv_count // 2) * rows, (1 + kv_count) * rows)
+        backs[d] = []
+        for i in range(2):
+            for k in range(kv_count):
+                at_row = (1 + k) * rows
+                if cuts[i] <= at_row < cuts[i + 1]:
+                    part_out[d - 1, at_row : at_row + rows, :] = theirs[2][k]
+            window = pl.ds(cuts[i], cuts[i + 1] - cuts[i])
+            copy = pltpu.make_async_remote_copy(
+                src_ref=part_out.at[d - 1, window],
+                dst_ref=part_in.at[d - 1, window],
+                send_sem=back_send.at[i, d - 1],
+                recv_sem=back_recv.at[i, d - 1],
+                device_id=at(-d),
+                device_id_type=MESH,
+            )
+            copy.start()
+            backs[d].append(copy)
+
+    for d in order:
+        for copy in backs[d]:
+            copy.wait_recv()
+        for k in range(kv_count):
+            part_peak = part_in[d - 1, :rows, 2 * k : 2 * k + 1]
+            part_total = part_in[d - 1, :rows, 2 * k + 1 : 2 * k + 2]
             peak = jnp.maximum(peaks[k], part_peak)
             factor = jnp.exp(peaks[k] - peak)
             part_factor = jnp.exp(part_peak - peak)
             peaks[k] = peak
             totals[k] = totals[k] * factor + part_total * part_factor
-            sums[k] = sums[k] * factor + part_in[d - 1, k * rows : (k + 1) * rows, :] * part_factor
+            sums[k] = sums[k] * factor + part_in[d - 1, (k + 1) * rows : (k + 2) * rows, :] * part_factor
     for k in range(kv_count):
         out_ref[k * rows : (k + 1) * rows, :] = (sums[k] / totals[k]).astype(out_ref.dtype)
     for d in order:
         for copy in asks[d]:
             copy.wait_send()
-        backs[d].wait_send()
+        for copy in backs[d]:
+            copy.wait_send()
 
 
 def body(queries, new_kv, kv_pages, page_index, page_owner, seq_pages):
@@ -229,8 +239,8 @@
             pltpu.SemaphoreType.DMA((5,)),
             pltpu.SemaphoreType.DMA((2, away)),
             pltpu.SemaphoreType.DMA((2, away)),
-            pltpu.SemaphoreType.DMA((away,)),
-            pltpu.SemaphoreType.DMA((away,)),
+            pltpu.SemaphoreType.DMA((2, away)),
+            pltpu.SemaphoreType.DMA((2, away)),
         ],
         compiler_params=pltpu.CompilerParams(collective_id=0, has_side_effects=True),
     )(q, new_kv, kv_pages, page_index, page_owner, seq_pages.reshape(1, seq_count))

time: 13.4 us -> 13.5 us (level)
  no operation moved by 1% of the time
where the time goes in v5:
time: 13.5 us; the launch traced here: 13.3 us
  Pallas kernels  12.7 us (94%)
  local copies, waits for them, and re-layouts  0.61 us (5%)
    pallas_call x1, Pallas kernels, body(): pl.pallas_call(functools.partial(kernel, n, seq_count, most_pages, capaci...  12.7 us
    unnamed x1, local copies, waits for them, and re-layouts  0.61 us

profile of v5, /device:TPU:0, one launch (start us, length us, event | category | flops | bytes accessed | tf_op | source)
XLA Modules:
  0.0 13.3 jit_solution(660818881487821515)
XLA Ops:
  0.0 12.7 %shard_map.64 = bf16[64,128]{1,0:T(8,128)(2,1)S(1)} custom-call(bf16[64,128]{1,0:T(8,128)(2,1)} %bitcast.12, bf16[2,2,512]{2,1,0:T(2,128)(2,1)} %fresh_ref.1, bf16[8,2,256,512]{3,2,1,0:T(8,128)(2,1)} %kv_ref.1, s32[2,4]{1,0:T(2,128)} %places_ref.1, s32[2,4]{1,0:T(2,128)} %owners_ref.1, s32[1,2]{1,0:T(1,128)} %bitcast.13), custom_call_target="tpu_custom_call" | custom-call | tf_op jit(solution)/shard_map/pallas_call | solution.py:218
  12.7 0.6 %copy.10 = bf16[2,4096]{1,0:T(2,128)(2,1)} copy(bf16[2,4096]{1,0:T(2,128)(2,1)S(1)} %bitcast.11) | data formatting | bytes 32768
